TPU v7x, 32 devices: a whole 2x2x4 slice. The times are simulated.
32 devices in a mesh: seq: 16 (over z, x, core), row: 2 (over y).
Axes of the slice: x: 2, y: 2, z: 4, core: 2. Of those that a mesh axis runs over, the one named last changes fastest.
Arguments:
- patch_queries: bfloat16 [2048, 2048], P('seq', 'row'), may hold values from -15 to 15
- patch_keys: bfloat16 [2048, 2048], P('seq', 'row'), may hold values from -15 to 15
- patch_values: bfloat16 [2048, 2048], P('seq', 'row'), may hold values from -6 to 6
- patch_tasks: int32 [2048], P('seq'), may hold values from 0 to 7
- residual: bfloat16 [2048, 2048], P('seq', 'row'), may hold values from -6 to 6
- output_weight: bfloat16 [2048, 2048], P('row'), may hold values from -0.5 to 0.5
- global_down: bfloat16 [2048, 16], P('row'), may hold values from -0.5 to 0.5
- global_up: bfloat16 [16, 2048], P(None, 'row'), may hold values from -1.5 to 1.5
- global_scales: float32 [8, 16], replicated, may hold values from 0.25 to 4
- local_weight: bfloat16 [2048, 512], P('row'), may hold values from -0.125 to 0.125
- byte_ids: int32 [16384], P('seq'), may hold values from 0 to 255
- byte_table: bfloat16 [256, 512], replicated, may hold values from -6 to 6
- position_table: bfloat16 [8, 512], replicated, may hold values from -6 to 6
- norm_gain: float32 [512], replicated, may hold values from 0.5 to 1.5
- hidden_in: bfloat16 [2048, 512], P('row', 'seq'), may hold values from -0.25 to 0.25
- hidden_out: bfloat16 [2048, 512], P('row', 'seq'), may hold values from -0.125 to 0.125
- local_down: bfloat16 [512, 16], replicated, may hold values from -0.25 to 0.25
- local_up: bfloat16 [16, 2048], P(None, 'row'), may hold values from -1.5 to 1.5
- local_scales: float32 [8, 16], replicated, may hold values from 0.25 to 4
- cotangent: bfloat16 [16384, 512], P(('seq', 'row')), may hold values from -6 to 6
Outputs:
- grad_global_down: float32 [2048, 16], P('row')
- grad_global_up: float32 [16, 2048], P(None, 'row')
- grad_global_scales: float32 [8, 16], replicated
- grad_local_down: float32 [512, 16], replicated
- grad_local_up: float32 [16, 2048], P(None, 'row')
- grad_local_scales: float32 [8, 16], replicated
All inputs are finite; a program needn't handle non-finite values.
Results may differ from a plain program's by a relative error of at most 0.028.
Values may be sent and summed in bfloat16 or wider, within the bound.
A program may use at most 64 MiB of HBM per device.

v0:
```python
import math
import jax
import jax.numpy as jnp
from jax import lax
from jax.sharding import PartitionSpec as P

HEAD = 128
VOCAB = 256
PATCH = 8
TASKS = 8


def contract(left, right, left_dim, right_dim):
    return lax.dot_general(
        left, right, (((left_dim,), (right_dim,)), ((), ())), preferred_element_type=jnp.float32
    )


def select_rows(table, tasks):
    picks = (tasks[:, None] == jnp.arange(table.shape[0], dtype=jnp.int32)[None, :]).astype(
        jnp.float32
    )
    return jnp.dot(picks, table, precision=lax.Precision.HIGHEST)


def task_totals(tasks, values):
    picks = (tasks[:, None] == jnp.arange(TASKS, dtype=jnp.int32)[None, :]).astype(jnp.float32)
    return lax.dot_general(picks, values, (((0,), (0,)), ((), ())), precision=lax.Precision.HIGHEST)


def gelu_slope(upper):
    cumulative = 0.5 * (1.0 + lax.erf(upper * 0.7071067811865476))
    density = jnp.exp(-0.5 * upper * upper) * 0.3989422804014327
    return cumulative + upper * density


def local_inputs(
    identities, projected, tasks, byte_table, position_table, norm_gain, local_down, local_scales
):
    count = identities.shape[0]
    picks = (identities[:, None] == jnp.arange(VOCAB, dtype=jnp.int32)[None, :]).astype(
        jnp.bfloat16
    )
    embedded = jnp.dot(picks, byte_table, preferred_element_type=jnp.float32)
    patches = count // PATCH
    inputs = (
        embedded.reshape(patches, PATCH, -1)
        + position_table.astype(jnp.float32)[None]
        + projected.astype(jnp.float32)[:, None, :]
    )
    inputs = inputs.reshape(count, -1)
    inverse = lax.rsqrt(jnp.mean(inputs * inputs, axis=1, keepdims=True) + 1e-06)
    normed = (inputs * inverse * norm_gain).astype(jnp.bfloat16)
    lowered = jnp.dot(normed, local_down, preferred_element_type=jnp.float32)
    byte_tasks = jnp.repeat(tasks, PATCH)
    scales = select_rows(local_scales, byte_tasks)
    shrunk = (lowered * scales).astype(jnp.bfloat16)
    return (inputs, inverse, normed, lowered, scales, shrunk, byte_tasks)


def keep_state(current):
    return current


def update_state(state, query_rows, first, key_heads, value_heads, key_places, scale):
    running_max, running_sum, running_out = state
    count = query_rows.shape[0]
    heads = key_heads.shape[1]
    query_heads = query_rows.reshape(count, heads, HEAD)
    scores = (
        jnp.einsum("qhd,khd->hqk", query_heads, key_heads, preferred_element_type=jnp.float32)
        * scale
    )
    query_places = first + jnp.arange(count, dtype=jnp.int32)
    allowed = key_places[None, :] <= query_places[:, None]
    scores = jnp.where(allowed[None], scores, -1e30)
    new_max = jnp.maximum(running_max, jnp.max(scores, axis=2))
    weights = jnp.where(allowed[None], jnp.exp(scores - new_max[:, :, None]), 0.0)
    shrink = jnp.exp(running_max - new_max)
    running_sum = running_sum * shrink + jnp.sum(weights, axis=2)
    mixed = jnp.einsum(
        "hqk,khd->qhd",
        weights.astype(jnp.bfloat16),
        value_heads,
        preferred_element_type=jnp.float32,
    )
    running_out = running_out * jnp.transpose(shrink)[:, :, None] + mixed
    return (new_max, running_sum, running_out)


def finish_state(state):
    running_max, running_sum, running_out = state
    result = running_out / jnp.transpose(running_sum)[:, :, None]
    return result.reshape(result.shape[0], -1).astype(jnp.bfloat16)


def body(
    patch_queries,
    patch_keys,
    patch_values,
    patch_tasks,
    residual,
    output_weight,
    global_down,
    global_up,
    global_scales,
    local_weight,
    byte_ids,
    byte_table,
    position_table,
    norm_gain,
    hidden_in,
    hidden_out,
    local_down,
    local_up,
    local_scales,
    cotangent,
):
    rows = patch_queries.shape[0]
    width = patch_queries.shape[1]
    heads = width // HEAD
    row_count = lax.axis_size("row")
    seq_index = lax.axis_index("seq")
    row_index = lax.axis_index("row")
    scale = 1.0 / math.sqrt(HEAD)
    own_first = seq_index * rows
    groups = [(patch_queries, own_first)]

    def visit(state, query_rows, first, key_heads, value_heads, key_places):

        def refresh(current):
            return update_state(
                current, query_rows, first, key_heads, value_heads, key_places, scale
            )

        return lax.cond(
            key_places[0] <= first + query_rows.shape[0] - 1, refresh, keep_state, state
        )

    initial = tuple(
        (
            (
                jnp.full((heads, query_rows.shape[0]), -1e30, jnp.float32),
                jnp.zeros((heads, query_rows.shape[0]), jnp.float32),
                jnp.zeros((query_rows.shape[0], heads, HEAD), jnp.float32),
            )
            for query_rows, first in groups
        )
    )
    key_piece = lax.all_gather(patch_keys, "seq", axis=0, tiled=True)
    value_piece = lax.all_gather(patch_values, "seq", axis=0, tiled=True)
    count = key_piece.shape[0]
    span = math.gcd(count, 1024)

    def one_span(index, states):
        offset = index * span
        key_heads = lax.dynamic_slice_in_dim(key_piece, offset, span, 0).reshape(span, heads, HEAD)
        value_heads = lax.dynamic_slice_in_dim(value_piece, offset, span, 0).reshape(
            span, heads, HEAD
        )
        key_places = offset + jnp.arange(span, dtype=jnp.int32)
        updated = []
        for (query_rows, first), state in zip(groups, states):
            updated.append(visit(state, query_rows, first, key_heads, value_heads, key_places))
        return tuple(updated)

    states = lax.fori_loop(0, count // span, one_span, initial)
    outputs = [finish_state(state) for state in states]
    attended = outputs[0]
    reduced = lax.psum(jnp.dot(attended, global_down, preferred_element_type=jnp.float32), "row")
    task_scales = select_rows(global_scales, patch_tasks)
    scaled = (reduced * task_scales).astype(jnp.bfloat16)
    mixed = lax.psum_scatter(
        contract(output_weight, attended, 0, 1).astype(jnp.bfloat16),
        "row",
        scatter_dimension=0,
        tiled=True,
    ).astype(jnp.float32)
    mixed = mixed + jnp.transpose(residual.astype(jnp.float32)) + contract(global_up, scaled, 0, 1)
    mixed_b = mixed.astype(jnp.bfloat16)
    own_patches = rows // row_count
    own_bytes = own_patches * PATCH
    rows_in, rows_out = (
        lax.all_gather(hidden_in, "seq", axis=1, tiled=True),
        lax.all_gather(hidden_out, "seq", axis=1, tiled=True),
    )
    partial_value = contract(mixed_b, local_weight, 0, 0)
    projected = lax.psum(partial_value.astype(jnp.bfloat16), "row")
    every = local_inputs(
        byte_ids,
        projected,
        patch_tasks,
        byte_table,
        position_table,
        norm_gain,
        local_down,
        local_scales,
    )
    normed_all = every[2]
    shrunk_all = every[5]
    cotangent_all = lax.all_gather(cotangent, "row", axis=0, tiled=True)
    inputs, inverse, normed, lowered, scales, shrunk, byte_tasks = [
        lax.dynamic_slice_in_dim(value, row_index * own_bytes, own_bytes, 0) for value in every
    ]
    upper = contract(normed_all, rows_in, 1, 1) + jnp.dot(
        shrunk_all, local_up, preferred_element_type=jnp.float32
    )
    through = contract(cotangent_all, rows_out, 1, 1)
    grown = (through * gelu_slope(upper)).astype(jnp.bfloat16)
    grad_local_up = contract(shrunk_all, grown, 0, 0)
    back_norm, back_rank = (
        lax.psum_scatter(
            jnp.dot(grown, rows_in, preferred_element_type=jnp.float32).astype(jnp.bfloat16),
            "row",
            scatter_dimension=0,
            tiled=True,
        ).astype(jnp.float32),
        lax.psum_scatter(
            contract(grown, local_up, 1, 1).astype(jnp.bfloat16),
            "row",
            scatter_dimension=0,
            tiled=True,
        ).astype(jnp.float32),
    )
    grad_local_scales = task_totals(byte_tasks, back_rank * lowered)
    moved = (back_rank * scales).astype(jnp.bfloat16)
    grad_local_down = contract(normed, moved, 0, 0)
    back_total = back_norm + contract(moved, local_down, 1, 1)
    gained = back_total * norm_gain
    average = jnp.mean(gained * inputs, axis=1, keepdims=True)
    back_inputs = cotangent.astype(jnp.float32) + inverse * (
        gained - inputs * inverse * inverse * average
    )
    patch_grad = back_inputs.reshape(own_patches, PATCH, -1).sum(axis=1).astype(jnp.bfloat16)
    back_mixed = contract(
        lax.all_gather(patch_grad, "row", axis=0, tiled=True), local_weight, 1, 1
    ).astype(jnp.bfloat16)
    grad_global_up = contract(scaled, back_mixed, 0, 0)
    back_scaled = lax.psum(contract(back_mixed, global_up, 1, 1), "row")
    grad_global_scales = task_totals(patch_tasks, back_scaled * reduced)
    back_reduced = (back_scaled * task_scales).astype(jnp.bfloat16)
    grad_global_down = contract(attended, back_reduced, 0, 0)
    grad_global_down, grad_global_up, grad_global_scales, grad_local_up = lax.psum(
        (grad_global_down, grad_global_up, grad_global_scales, grad_local_up), "seq"
    )
    grad_local_down, grad_local_scales = lax.psum(
        (grad_local_down, grad_local_scales), ("seq", "row")
    )
    return (
        grad_global_down,
        grad_global_up,
        grad_global_scales,
        grad_local_down,
        grad_local_up,
        grad_local_scales,
    )


def solution(mesh):
    placed = (
        P("seq", "row"),
        P("seq", "row"),
        P("seq", "row"),
        P("seq"),
        P("seq", "row"),
        P("row", None),
        P("row", None),
        P(None, "row"),
        P(),
        P("row", None),
        P("seq"),
        P(),
        P(),
        P(),
        P("row", "seq"),
        P("row", "seq"),
        P(),
        P(None, "row"),
        P(),
        P(("seq", "row"), None),
    )
    return jax.shard_map(
        body,
        mesh=mesh,
        in_specs=placed,
        out_specs=(P("row", None), P(None, "row"), P(), P(), P(None, "row"), P()),
        check_vma=False,
    )
```

profile of v0, /device:TPU:0, one launch (start us, length us, event | category | flops | bytes accessed | tf_op | source)
XLA Modules:
  0.0 456.6 jit_solution(17964355863576185190)
XLA Ops:
  7.2 1.9 copy.32
  11.1 54.3 %all-gather.6.cloned.1.call-done = bf16[2048,1024]{0,1:T(8,128)(2,1)} async-done(((bf16[128,1024]{0,1:T(8,128)(2,1)}), bf16[2048,1024]{0,1:T(8,128)(2,1)}) %all-gather.6.cloned.1.call-update) | async-done | bytes 4194320 | tf_op jit(solution)/shard_map/all_gather | solution.py:150
  65.4 52.8 %all-gather.8.cloned.1.call-done = bf16[2048,1024]{0,1:T(8,128)(2,1)} async-done(((bf16[128,1024]{0,1:T(8,128)(2,1)}), bf16[2048,1024]{0,1:T(8,128)(2,1)}) %all-gather.8.cloned.1.call-update) | async-done | bytes 4194320 | tf_op jit(solution)/shard_map/all_gather | solution.py:151
  118.3 9.3 %while.19 = (s32[]{:T(128)}, f32[8,128]{1,0:T(8,128)S(1)}, f32[8,128]{1,0:T(8,128)S(1)}, f32[128,8,128]{2,0,1:T(8,128)S(1)}, s32[]{:T(128)}, /*index=5*/s32[]{:T...) while((s32[]{:T(128)}, f32[8,128]{1,0:T(8,128)S(1)}, ...), condition=%wide.region_5.6_spmd, body=%wide.region_0.5_spmd.sunk | while | flops 550899840 | bytes 28124504 | solution.py:167
  119.5 6.9 %conditional.2 = ((f32[8,128]{1,0:T(8,128)S(1)}, f32[8,128]{1,0:T(8,128)S(1)}, f32[128,8,128]{2,0,1:T(8,128)S(1)})) conditional(s32[]{:T(128)} %convert_element_type.155, (f32[8,128]{1,0:T(8,128)S(1)}, f32[8,128]{1,0:T(8,128)S(1)}, f32[128,8,128]{2,0,1:T(8,128)S(1)}) %tuple.65, (s32[1024]{0:T(1024)S(1)}, s32[]{:T(128)}, s32[]{:T(128)}, ...), branch_computations={%region_1.0_spmd, %region_2.4_spmd} | conditional | flops 550898816 | bytes 28120166 | solution.py:136
  119.5 2.7 constant_dynamic-slice_fusion
  128.0 3.7 fusion.29
  133.1 5.0 %psum.63 = f32[128,16]{0,1:T(8,128)S(1)} all-reduce(f32[128,16]{0,1:T(8,128)S(1)} %fusion.65), channel_id=1, replica_groups=mesh['seq'=16,'row'=2] {'row'}, use_global_device_ids=true, to_apply=%region_7.8 | all-reduce | flops 2048 | bytes 16384 | tf_op jit(solution)/shard_map/psum | solution.py:170
  139.0 12.6 %reduce-scatter.4.cloned.1.call-done = bf16[1024,128]{0,1:T(8,128)(2,1)} async-done(((bf16[2048,128]{0,1:T(8,128)(2,1)}), bf16[1024,128]{0,1:T(8,128)(2,1)}) %reduce-scatter.4.cloned.1.call-update) | async-done | bytes 262160 | tf_op jit(solution)/shard_map/reduce_scatter | solution.py:173
  151.6 2.1 fusion.34
  155.2 19.1 %all-gather.10.cloned.1.call-done = bf16[1024,512]{1,0:T(8,128)(2,1)} async-done(((bf16[512,512]{1,0:T(8,128)(2,1)}), bf16[1024,512]{1,0:T(8,128)(2,1)}) %all-gather.10.cloned.1.call-update) | async-done | bytes 1048592 | tf_op jit(solution)/shard_map/all_gather | solution.py:201
  174.3 39.9 %all-gather.12.cloned.1.call-done = bf16[1024,512]{0,1:T(8,128)(2,1)} async-done(((bf16[1024,32]{0,1:T(8,128)(2,1)}), bf16[1024,512]{0,1:T(8,128)(2,1)}) %all-gather.12.cloned.1.call-update) | async-done | bytes 1048592 | tf_op jit(solution)/shard_map/all_gather | solution.py:185
  214.2 4.7 %fusion.60 = f32[1024,1024]{1,0:T(8,128)} fusion(bf16[1024,512]{1,0:T(8,128)(2,1)} %all-gather.10.cloned.1.call-done, bf16[1024,512]{0,1:T(8,128)(2,1)} %all-gather.12.cloned.1.call-done), kind=kOutput, calls=%fused_computation.86 | convolution fusion | flops 1073741824 | bytes 6291456 | tf_op jit(solution)/shard_map/dot_general | solution.py:14
  218.9 17.9 %all-reduce.5.cloned.1.call-done = bf16[128,512]{1,0:T(8,128)(2,1)} async-done(((bf16[128,512]{1,0:T(8,128)(2,1)}), bf16[128,512]{1,0:T(8,128)(2,1)}) %all-reduce.5.cloned.1.call-update) | async-done | bytes 131088 | tf_op jit(solution)/shard_map/psum | solution.py:188
  242.3 34.6 %all-gather.14.cloned.1.call-done = bf16[1024,512]{0,1:T(8,128)(2,1)} async-done(((bf16[1024,32]{0,1:T(8,128)(2,1)}), bf16[1024,512]{0,1:T(8,128)(2,1)}) %all-gather.14.cloned.1.call-update) | async-done | bytes 1048592 | tf_op jit(solution)/shard_map/all_gather | solution.py:184
  276.8 2.9 fusion.61
  279.8 2.3 fusion.28
  284.9 4.1 convolution_convert_fusion.1
  291.8 2.6 fusion.64
  297.4 40.2 %all-reduce = (f32[512,16]{0,1:T(8,128)}, f32[8,16]{1,0:T(8,128)}) all-reduce(f32[512,16]{0,1:T(8,128)S(1)} %fusion.36, f32[8,16]{1,0:T(8,128)} %fusion.43), channel_id=1, replica_groups=mesh['seq'=16,'row'=2] {'seq','row'}, use_global_device_ids=true, to_apply=%region_18.19 | all-reduce | flops 8320 | bytes 66560 | tf_op jit(solution)/shard_map/psum | solution.py:246
  340.8 5.2 %all_gather.23 = bf16[128,512]{1,0:T(8,128)(2,1)S(1)} all-gather(bf16[64,512]{1,0:T(8,128)(2,1)S(1)} %bitcast_reduce_fusion), channel_id=1, replica_groups=mesh['seq'=16,'row'=2] {'row'}, dimensions={0}, use_global_device_ids=true | all-gather | bytes 196608 | tf_op jit(solution)/shard_map/all_gather | solution.py:236
  347.5 5.0 %psum.65 = f32[128,16]{0,1:T(8,128)S(1)} all-reduce(f32[128,16]{0,1:T(8,128)S(1)} %fusion.62), channel_id=1, replica_groups=mesh['seq'=16,'row'=2] {'row'}, use_global_device_ids=true, to_apply=%region_14.15 | all-reduce | flops 2048 | bytes 16384 | tf_op jit(solution)/shard_map/psum | solution.py:239
  353.5 30.1 %psum.68 = f32[8,16]{1,0:T(8,128)} all-reduce(f32[8,16]{1,0:T(8,128)S(1)} %fusion.49), channel_id=1, replica_groups=mesh['seq'=16,'row'=2] {'seq'}, use_global_device_ids=true, to_apply=%region_17.18 | all-reduce | flops 128 | bytes 1024 | tf_op jit(solution)/shard_map/psum | solution.py:243
  383.6 61.7 %all-reduce.7.cloned.1.call-done = (f32[1024,16]{0,1:T(8,128)}, f32[16,1024]{1,0:T(8,128)}, f32[16,1024]{1,0:T(8,128)}) async-done(((f32[1024,16]{0,1:T(8,128)}, f32[16,1024]{1,0:T(8,128)}, f32[16,1024]{1,0:T(8,128)}), (f32[1024,16]{0,1:T(8,128)}, f32[16,1024]{1,0:T(8,128)}, f32[16,1024]{1,0:T(8,128)})) %all-reduce.7.cloned.1.call-update) | async-done | bytes 196624 | tf_op jit(solution)/shard_map/psum | solution.py:243
  (114 shorter events, 35.2 us)
Async XLA Ops:
  7.2 144.4 %copy-start = (bf16[1024,512]{1,0:T(8,128)(2,1)S(1)}, bf16[1024,512]{1,0:T(8,128)(2,1)}, u32[]{:S(2)}) copy-start(bf16[1024,512]{1,0:T(8,128)(2,1)} %param.33) | copy-start | bytes 3145732
  7.2 58.2 %all-gather.6.cloned.1.call-start = ((), (), s32[]{:S(2)}) async-start(), calls=%async_computation.3 | async-start | bytes 4456448 | tf_op jit(solution)/shard_map/all_gather | solution.py:150
  9.1 109.1 %all-gather.8.cloned.1.call-start = ((), (), s32[]{:S(2)}) async-start(), calls=%async_computation.4 | async-start | bytes 4456448 | tf_op jit(solution)/shard_map/all_gather | solution.py:151
  11.0 140.6 %reduce-scatter.4.cloned.1.call-start = ((), (), s32[]{:S(2)}) async-start(), calls=%async_computation.5 | async-start | bytes 786432 | tf_op jit(solution)/shard_map/reduce_scatter | solution.py:173
  127.6 10.5 %copy-start.18 = (s32[128]{0:T(128)S(1)}, s32[128]{0:T(128)}, u32[]{:S(2)}) copy-start(s32[128]{0:T(128)} %param.27) | copy-start | bytes 1540
  127.7 23.9 %copy-start.4 = (bf16[128,1024]{1,0:T(8,128)(2,1)S(1)}, bf16[128,1024]{1,0:T(8,128)(2,1)}, u32[]{:S(2)}) copy-start(bf16[128,1024]{1,0:T(8,128)(2,1)} %param.28) | copy-start | bytes 786436
  127.7 23.9 %copy-start.5 = (bf16[16,1024]{1,0:T(8,128)(2,1)S(1)}, bf16[16,1024]{1,0:T(8,128)(2,1)}, u32[]{:S(2)}) copy-start(bf16[16,1024]{1,0:T(8,128)(2,1)} %param.31) | copy-start | bytes 98308
  127.9 26.5 %copy-start.13 = (bf16[8,512]{1,0:T(8,128)(2,1)S(1)}, bf16[8,512]{1,0:T(8,128)(2,1)}, u32[]{:S(2)}) copy-start(bf16[8,512]{1,0:T(8,128)(2,1)} %param.36) | copy-start | bytes 24580
  128.0 26.7 %copy-start.21 = (f32[8,16]{1,0:T(8,128)S(1)}, f32[8,16]{1,0:T(8,128)}, u32[]{:S(2)}) copy-start(f32[8,16]{1,0:T(8,128)} %param.42) | copy-start | bytes 1540
  131.7 42.6 %all-gather.10.cloned.1.call-start = ((), (), s32[]{:S(2)}) async-start(), calls=%async_computation.7 | async-start | bytes 1572864 | tf_op jit(solution)/shard_map/all_gather | solution.py:201
  132.3 81.9 %all-gather.12.cloned.1.call-start = ((), (), s32[]{:S(2)}) async-start(), calls=%async_computation.8 | async-start | bytes 1114112 | tf_op jit(solution)/shard_map/all_gather | solution.py:185
  132.9 103.9 %all-reduce.5.cloned.1.call-start = ((), (), s32[]{:S(2)}) async-start(), calls=%async_computation.6 | async-start | bytes 262144 | tf_op jit(solution)/shard_map/psum | solution.py:188
  138.1 80.8 %copy-start.15 = (f32[128,16]{0,1:T(8,128)}, f32[128,16]{0,1:T(8,128)S(1)}, u32[]{:S(2)}) copy-start(f32[128,16]{0,1:T(8,128)S(1)} %psum.63) | copy-start | bytes 24580
  139.0 15.6 %copy-start.10 = (bf16[128,16]{0,1:T(8,128)(2,1)}, bf16[128,16]{0,1:T(8,128)(2,1)S(1)}, u32[]{:S(2)}) copy-start(bf16[128,16]{0,1:T(8,128)(2,1)S(1)} %get-tuple-element.359) | copy-start | bytes 12292
  153.7 123.2 %all-gather.14.cloned.1.call-start = ((), (), s32[]{:S(2)}) async-start(), calls=%async_computation.9 | async-start | bytes 1114112 | tf_op jit(solution)/shard_map/all_gather | solution.py:184
  154.4 140.0 %reduce-scatter.8.cloned.1.call-start = ((), (), s32[]{:S(2)}) async-start(), calls=%async_computation.11 | async-start | bytes 49152 | tf_op jit(solution)/shard_map/reduce_scatter | solution.py:218
  154.7 64.2 %copy-start.12 = (s32[1024]{0:T(1024)}, s32[1024]{0:T(1024)S(1)}, u32[]{:S(2)}) copy-start(s32[1024]{0:T(1024)S(1)} %eq.32) | copy-start | bytes 12292
  155.2 84.8 %copy-start.17 = (f32[512]{0:T(512)S(1)}, f32[512]{0:T(512)}, u32[]{:S(2)}) copy-start(f32[512]{0:T(512)} %param.37) | copy-start | bytes 6148
  218.9 22.3 %copy-start.6 = (bf16[512,16]{0,1:T(8,128)(2,1)S(1)}, bf16[512,16]{0,1:T(8,128)(2,1)}, u32[]{:S(2)}) copy-start(bf16[512,16]{0,1:T(8,128)(2,1)} %param.40) | copy-start | bytes 49156
  284.7 52.9 %reduce-scatter.6.cloned.1.call-start = ((), (), s32[]{:S(2)}) async-start(), calls=%async_computation.10 | async-start | bytes 1572864 | tf_op jit(solution)/shard_map/reduce_scatter | solution.py:212
  289.1 156.2 %all-reduce.7.cloned.1.call-start = ((), (), s32[]{:S(2)}) async-start(), calls=%async_computation.12 | async-start | bytes 393216 | tf_op jit(solution)/shard_map/psum | solution.py:243
  337.6 14.8 %copy-start.14 = (f32[128,16]{0,1:T(8,128)S(1)}, f32[128,16]{0,1:T(8,128)}, u32[]{:S(2)}) copy-start(f32[128,16]{0,1:T(8,128)} %get-tuple-element.360) | copy-start | bytes 24580
  337.6 15.7 %copy-start.16 = (f32[128,16]{0,1:T(8,128)S(1)}, f32[128,16]{0,1:T(8,128)}, u32[]{:S(2)}) copy-start(f32[128,16]{0,1:T(8,128)} %copy-done.15) | copy-start | bytes 24580
  337.6 15.7 %copy-start.19 = (s32[128]{0:T(128)S(1)}, s32[128]{0:T(128)}, u32[]{:S(2)}) copy-start(s32[128]{0:T(128)} %param.27) | copy-start | bytes 1540
  (9 other events, 36.6 us)
Sparse Core Ops, SparseCore 0:
  10.1 55.1 all-gather.5
  67.5 50.6 all-gather.7
  131.9 19.6 reduce-scatter.3
  153.0 21.2 all-gather.9
  176.3 37.8 all-gather.11
  216.3 20.4 all-reduce.4
  239.0 37.8 all-gather.13
  284.8 8.9 reduce-scatter.7
  296.1 20.9 reduce-scatter.5
  353.4 91.8 all-reduce.6
where the time goes:
time: 457 us
  waiting for transfers between devices  295 us (65%)
  blocking collectives  85.4 us (19%)
  matrix products  37.7 us (8%)
  local copies, waits for them, and re-layouts  17.9 us (4%)
  between operations  14.5 us (3%)
    psum x1, waiting for transfers between devices, body(): lax.psum((grad_global_down, grad_global_up, grad_global_scales, grad_loca...  61.7 us
    all_gather x1, waiting for transfers between devices, body(): key_piece = lax.all_gather(patch_keys, 'seq', axis=0, tiled=True)  54.3 us
    all_gather x1, waiting for transfers between devices, body(): value_piece = lax.all_gather(patch_values, 'seq', axis=0, tiled=True)  52.8 us
    psum x1, blocking collectives, body(): lax.psum((grad_local_down, grad_local_scales), ('seq', 'row'))  40.2 us
    all_gather x1, waiting for transfers between devices, body(): lax.all_gather(hidden_out, 'seq', axis=1, tiled=True)  39.9 us
    all_gather x1, waiting for transfers between devices, body(): lax.all_gather(hidden_in, 'seq', axis=1, tiled=True)  34.6 us
    psum x1, blocking collectives, body(): lax.psum((grad_global_down, grad_global_up, grad_global_scales, grad_loca...  30.1 us
    dot_general x12, matrix products, contract(): lax.dot_general(left, right, (((left_dim,), (right_dim,)), ((), ())), pre...  22.4 us
  transfers between devices with their start and end apart: 10, of which 8 were waited for; matrix products, arithmetic and copies ran while one was open for 6% of the time, Pallas kernels for 0%

commit v1 on v0

--- a/solution.py
+++ b/solution.py
@@ -147,8 +147,13 @@
             for query_rows, first in groups
         )
     )
-    key_piece = lax.all_gather(patch_keys, "seq", axis=0, tiled=True)
-    value_piece = lax.all_gather(patch_values, "seq", axis=0, tiled=True)
+    key_piece, value_piece = jnp.split(
+        lax.all_gather(
+            jnp.concatenate([patch_keys, patch_values], axis=1), "seq", axis=0, tiled=True
+        ),
+        [patch_keys.shape[1]],
+        axis=1,
+    )
     count = key_piece.shape[0]
     span = math.gcd(count, 1024)
 

time: 457 us -> 436 us (0.954)
  waiting for transfers between devices: 295 us -> 268 us
  local copies, waits for them, and re-layouts: 17.9 us -> 22.5 us
    all_gather x2 -> x1, waiting for transfers between devices: 107 us -> 80.5 us  [body(): lax.all_gather(jnp.concatenate([patch_keys, patch_values], axis=1), 'seq'...]
    split x0 -> x1, local copies, waits for them, and re-layouts: none -> 6.02 us  [body(): jnp.split(lax.all_gather(jnp.concatenate([patch_keys, patch_values], axis...]
    unnamed x49 -> x51, local copies, waits for them, and re-layouts: 11.1 us -> 9.72 us
  transfers between devices with their start and end apart: 10 -> 9, of which waited for: 8 -> 7; matrix products, arithmetic and copies ran while one was open for 6% -> 6% of each run, Pallas kernels for 0% -> 0%
where the time goes in v1:
time: 436 us; the launch traced here: 435 us
  waiting for transfers between devices  268 us (61%)
  blocking collectives  85.4 us (20%)
  matrix products  37.7 us (9%)
  local copies, waits for them, and re-layouts  22.5 us (5%)
  between operations  14.2 us (3%)
  other arithmetic  5 us (1%)
    all_gather x1, waiting for transfers between devices, body(): lax.all_gather(jnp.concatenate([patch_keys, patch_values], axis=1), 'seq'...  80.5 us
    psum x1, waiting for transfers between devices, body(): lax.psum((grad_global_down, grad_global_up, grad_global_scales, grad_loca...  61.8 us
    psum x1, blocking collectives, body(): lax.psum((grad_local_down, grad_local_scales), ('seq', 'row'))  40.2 us
    all_gather x1, waiting for transfers between devices, body(): lax.all_gather(hidden_out, 'seq', axis=1, tiled=True)  39.9 us
    all_gather x1, waiting for transfers between devices, body(): lax.all_gather(hidden_in, 'seq', axis=1, tiled=True)  34.5 us
    psum x1, blocking collectives, body(): lax.psum((grad_global_down, grad_global_up, grad_global_scales, grad_loca...  30.1 us
    dot_general x12, matrix products, contract(): lax.dot_general(left, right, (((left_dim,), (right_dim,)), ((), ())), pre...  22.4 us
    all_gather x1, waiting for transfers between devices, body(): cotangent_all = lax.all_gather(cotangent, 'row', axis=0, tiled=True)  19.3 us
  transfers between devices with their start and end apart: 9, of which 7 were waited for; matrix products, arithmetic and copies ran while one was open for 6% of the time, Pallas kernels for 0%

profile of v1, /device:TPU:0, one launch (start us, length us, event | category | flops | bytes accessed | tf_op | source)
XLA Modules:
  0.0 434.9 jit_solution(17133954023818256263)
XLA Ops:
  10.5 80.5 %all-gather.5.cloned.1.call-done = bf16[2048,2048]{0,1:T(8,128)(2,1)} async-done(((bf16[128,2048]{0,1:T(8,128)(2,1)}), bf16[2048,2048]{0,1:T(8,128)(2,1)}) %all-gather.5.cloned.1.call-update) | async-done | bytes 8388624 | tf_op jit(solution)/shard_map/all_gather | solution.py:151
  91.1 6.0 %fusion.60 = (bf16[2048,1024]{0,1:T(8,128)(2,1)}, bf16[2048,1024]{0,1:T(8,128)(2,1)}) fusion(bf16[2048,2048]{0,1:T(8,128)(2,1)} %all-gather.5.cloned.1.call-done), kind=kLoop, calls=%fused_computation.87 | loop fusion | bytes 16777216 | tf_op jit(solution)/shard_map/split | solution.py:150
  97.2 9.3 %while.19 = (s32[]{:T(128)}, f32[8,128]{1,0:T(8,128)S(1)}, f32[8,128]{1,0:T(8,128)S(1)}, f32[128,8,128]{2,0,1:T(8,128)S(1)}, s32[]{:T(128)}, /*index=5*/s32[]{:T...) while((s32[]{:T(128)}, f32[8,128]{1,0:T(8,128)S(1)}, ...), condition=%wide.region_5.6_spmd, body=%wide.region_0.5_spmd.sunk | while | flops 550899840 | bytes 27075900 | solution.py:172
  98.3 6.8 %conditional.2 = ((f32[8,128]{1,0:T(8,128)S(1)}, f32[8,128]{1,0:T(8,128)S(1)}, f32[128,8,128]{2,0,1:T(8,128)S(1)})) conditional(s32[]{:T(128)} %convert_element_type.155, (f32[8,128]{1,0:T(8,128)S(1)}, f32[8,128]{1,0:T(8,128)S(1)}, f32[128,8,128]{2,0,1:T(8,128)S(1)}) %tuple.66, (s32[1024]{0:T(1024)S(1)}, s32[]{:T(128)}, s32[]{:T(128)}, ...), branch_computations={%region_1.0_spmd, %region_2.4_spmd} | conditional | flops 550898816 | bytes 27071562 | solution.py:136
  98.4 2.7 constant_dynamic-slice_fusion
  106.8 3.8 fusion.29
  112.1 5.0 %psum.63 = f32[128,16]{0,1:T(8,128)S(1)} all-reduce(f32[128,16]{0,1:T(8,128)S(1)} %fusion.66), channel_id=1, replica_groups=mesh['seq'=16,'row'=2] {'row'}, use_global_device_ids=true, to_apply=%region_7.8 | all-reduce | flops 2048 | bytes 16384 | tf_op jit(solution)/shard_map/psum | solution.py:175
  117.9 12.4 %reduce-scatter.4.cloned.1.call-done = bf16[1024,128]{0,1:T(8,128)(2,1)} async-done(((bf16[2048,128]{0,1:T(8,128)(2,1)}), bf16[1024,128]{0,1:T(8,128)(2,1)}) %reduce-scatter.4.cloned.1.call-update) | async-done | bytes 262160 | tf_op jit(solution)/shard_map/reduce_scatter | solution.py:178
  130.3 2.1 fusion.34
  133.9 19.3 %all-gather.7.cloned.1.call-done = bf16[1024,512]{1,0:T(8,128)(2,1)} async-done(((bf16[512,512]{1,0:T(8,128)(2,1)}), bf16[1024,512]{1,0:T(8,128)(2,1)}) %all-gather.7.cloned.1.call-update) | async-done | bytes 1048592 | tf_op jit(solution)/shard_map/all_gather | solution.py:206
  153.2 39.9 %all-gather.9.cloned.1.call-done = bf16[1024,512]{0,1:T(8,128)(2,1)} async-done(((bf16[1024,32]{0,1:T(8,128)(2,1)}), bf16[1024,512]{0,1:T(8,128)(2,1)}) %all-gather.9.cloned.1.call-update) | async-done | bytes 1048592 | tf_op jit(solution)/shard_map/all_gather | solution.py:190
  193.1 4.7 %fusion.61 = f32[1024,1024]{1,0:T(8,128)} fusion(bf16[1024,512]{1,0:T(8,128)(2,1)} %all-gather.7.cloned.1.call-done, bf16[1024,512]{0,1:T(8,128)(2,1)} %all-gather.9.cloned.1.call-done), kind=kOutput, calls=%fused_computation.88 | convolution fusion | flops 1073741824 | bytes 6291456 | tf_op jit(solution)/shard_map/dot_general | solution.py:14
  197.8 17.9 %all-reduce.5.cloned.1.call-done = bf16[128,512]{1,0:T(8,128)(2,1)} async-done(((bf16[128,512]{1,0:T(8,128)(2,1)}), bf16[128,512]{1,0:T(8,128)(2,1)}) %all-reduce.5.cloned.1.call-update) | async-done | bytes 131088 | tf_op jit(solution)/shard_map/psum | solution.py:193
  221.1 34.5 %all-gather.11.cloned.1.call-done = bf16[1024,512]{0,1:T(8,128)(2,1)} async-done(((bf16[1024,32]{0,1:T(8,128)(2,1)}), bf16[1024,512]{0,1:T(8,128)(2,1)}) %all-gather.11.cloned.1.call-update) | async-done | bytes 1048592 | tf_op jit(solution)/shard_map/all_gather | solution.py:189
  255.6 2.9 fusion.62
  258.6 2.3 fusion.28
  263.5 4.1 convolution_convert_fusion.1
  270.4 2.6 fusion.65
  273.0 1.8 fusion.43
  276.0 40.2 %all-reduce = (f32[512,16]{0,1:T(8,128)}, f32[8,16]{1,0:T(8,128)}) all-reduce(f32[512,16]{0,1:T(8,128)S(1)} %fusion.36, f32[8,16]{1,0:T(8,128)} %fusion.43), channel_id=1, replica_groups=mesh['seq'=16,'row'=2] {'seq','row'}, use_global_device_ids=true, to_apply=%region_18.19 | all-reduce | flops 8320 | bytes 66560 | tf_op jit(solution)/shard_map/psum | solution.py:251
  319.4 5.2 %all_gather.19 = bf16[128,512]{1,0:T(8,128)(2,1)S(1)} all-gather(bf16[64,512]{1,0:T(8,128)(2,1)S(1)} %bitcast_reduce_fusion), channel_id=1, replica_groups=mesh['seq'=16,'row'=2] {'row'}, dimensions={0}, use_global_device_ids=true | all-gather | bytes 196608 | tf_op jit(solution)/shard_map/all_gather | solution.py:241
  326.0 5.0 %psum.65 = f32[128,16]{0,1:T(8,128)S(1)} all-reduce(f32[128,16]{0,1:T(8,128)S(1)} %fusion.63), channel_id=1, replica_groups=mesh['seq'=16,'row'=2] {'row'}, use_global_device_ids=true, to_apply=%region_14.15 | all-reduce | flops 2048 | bytes 16384 | tf_op jit(solution)/shard_map/psum | solution.py:244
  332.1 30.1 %psum.68 = f32[8,16]{1,0:T(8,128)} all-reduce(f32[8,16]{1,0:T(8,128)S(1)} %fusion.49), channel_id=1, replica_groups=mesh['seq'=16,'row'=2] {'seq'}, use_global_device_ids=true, to_apply=%region_17.18 | all-reduce | flops 128 | bytes 1024 | tf_op jit(solution)/shard_map/psum | solution.py:248
  362.2 61.8 %all-reduce.7.cloned.1.call-done = (f32[1024,16]{0,1:T(8,128)}, f32[16,1024]{1,0:T(8,128)}, f32[16,1024]{1,0:T(8,128)}) async-done(((f32[1024,16]{0,1:T(8,128)}, f32[16,1024]{1,0:T(8,128)}, f32[16,1024]{1,0:T(8,128)}), (f32[1024,16]{0,1:T(8,128)}, f32[16,1024]{1,0:T(8,128)}, f32[16,1024]{1,0:T(8,128)})) %all-reduce.7.cloned.1.call-update) | async-done | bytes 196624 | tf_op jit(solution)/shard_map/psum | solution.py:248
  (113 shorter events, 34.7 us)
Async XLA Ops:
  7.2 123.2 %copy-start = (bf16[1024,512]{1,0:T(8,128)(2,1)S(1)}, bf16[1024,512]{1,0:T(8,128)(2,1)}, u32[]{:S(2)}) copy-start(bf16[1024,512]{1,0:T(8,128)(2,1)} %param.33) | copy-start | bytes 3145732
  7.2 83.9 %all-gather.5.cloned.1.call-start = ((), (), s32[]{:S(2)}) async-start(), calls=%async_computation.3 | async-start | bytes 8912896 | tf_op jit(solution)/shard_map/all_gather | solution.py:151
  10.5 119.8 %reduce-scatter.4.cloned.1.call-start = ((), (), s32[]{:S(2)}) async-start(), calls=%async_computation.4 | async-start | bytes 786432 | tf_op jit(solution)/shard_map/reduce_scatter | solution.py:178
  10.5 86.6 %copy-start.2 = (bf16[128,1024]{1,0:T(8,128)(2,1)S(1)}, bf16[128,1024]{1,0:T(8,128)(2,1)}, u32[]{:S(2)}) copy-start(bf16[128,1024]{1,0:T(8,128)(2,1)} %param.24) | copy-start | bytes 786436
  106.4 10.6 %copy-start.18 = (s32[128]{0:T(128)S(1)}, s32[128]{0:T(128)}, u32[]{:S(2)}) copy-start(s32[128]{0:T(128)} %param.27) | copy-start | bytes 1540
  106.5 23.9 %copy-start.4 = (bf16[128,1024]{1,0:T(8,128)(2,1)S(1)}, bf16[128,1024]{1,0:T(8,128)(2,1)}, u32[]{:S(2)}) copy-start(bf16[128,1024]{1,0:T(8,128)(2,1)} %param.28) | copy-start | bytes 786436
  106.5 23.9 %copy-start.5 = (bf16[16,1024]{1,0:T(8,128)(2,1)S(1)}, bf16[16,1024]{1,0:T(8,128)(2,1)}, u32[]{:S(2)}) copy-start(bf16[16,1024]{1,0:T(8,128)(2,1)} %param.31) | copy-start | bytes 98308
  106.7 26.5 %copy-start.13 = (bf16[8,512]{1,0:T(8,128)(2,1)S(1)}, bf16[8,512]{1,0:T(8,128)(2,1)}, u32[]{:S(2)}) copy-start(bf16[8,512]{1,0:T(8,128)(2,1)} %param.36) | copy-start | bytes 24580
  106.8 26.7 %copy-start.21 = (f32[8,16]{1,0:T(8,128)S(1)}, f32[8,16]{1,0:T(8,128)}, u32[]{:S(2)}) copy-start(f32[8,16]{1,0:T(8,128)} %param.42) | copy-start | bytes 1540
  110.5 42.7 %all-gather.7.cloned.1.call-start = ((), (), s32[]{:S(2)}) async-start(), calls=%async_computation.6 | async-start | bytes 1572864 | tf_op jit(solution)/shard_map/all_gather | solution.py:206
  111.3 81.8 %all-gather.9.cloned.1.call-start = ((), (), s32[]{:S(2)}) async-start(), calls=%async_computation.7 | async-start | bytes 1114112 | tf_op jit(solution)/shard_map/all_gather | solution.py:190
  111.9 103.9 %all-reduce.5.cloned.1.call-start = ((), (), s32[]{:S(2)}) async-start(), calls=%async_computation.5 | async-start | bytes 262144 | tf_op jit(solution)/shard_map/psum | solution.py:193
  117.0 80.8 %copy-start.15 = (f32[128,16]{0,1:T(8,128)}, f32[128,16]{0,1:T(8,128)S(1)}, u32[]{:S(2)}) copy-start(f32[128,16]{0,1:T(8,128)S(1)} %psum.63) | copy-start | bytes 24580
  117.9 15.4 %copy-start.10 = (bf16[128,16]{0,1:T(8,128)(2,1)}, bf16[128,16]{0,1:T(8,128)(2,1)S(1)}, u32[]{:S(2)}) copy-start(bf16[128,16]{0,1:T(8,128)(2,1)S(1)} %get-tuple-element.361) | copy-start | bytes 12292
  132.4 123.2 %all-gather.11.cloned.1.call-start = ((), (), s32[]{:S(2)}) async-start(), calls=%async_computation.8 | async-start | bytes 1114112 | tf_op jit(solution)/shard_map/all_gather | solution.py:189
  133.0 140.0 %reduce-scatter.8.cloned.1.call-start = ((), (), s32[]{:S(2)}) async-start(), calls=%async_computation.10 | async-start | bytes 49152 | tf_op jit(solution)/shard_map/reduce_scatter | solution.py:223
  133.4 64.4 %copy-start.12 = (s32[1024]{0:T(1024)}, s32[1024]{0:T(1024)S(1)}, u32[]{:S(2)}) copy-start(s32[1024]{0:T(1024)S(1)} %eq.32) | copy-start | bytes 12292
  133.9 85.0 %copy-start.17 = (f32[512]{0:T(512)S(1)}, f32[512]{0:T(512)}, u32[]{:S(2)}) copy-start(f32[512]{0:T(512)} %param.37) | copy-start | bytes 6148
  197.8 22.3 %copy-start.6 = (bf16[512,16]{0,1:T(8,128)(2,1)S(1)}, bf16[512,16]{0,1:T(8,128)(2,1)}, u32[]{:S(2)}) copy-start(bf16[512,16]{0,1:T(8,128)(2,1)} %param.40) | copy-start | bytes 49156
  263.5 52.8 %reduce-scatter.6.cloned.1.call-start = ((), (), s32[]{:S(2)}) async-start(), calls=%async_computation.9 | async-start | bytes 1572864 | tf_op jit(solution)/shard_map/reduce_scatter | solution.py:217
  267.7 156.3 %all-reduce.7.cloned.1.call-start = ((), (), s32[]{:S(2)}) async-start(), calls=%async_computation.11 | async-start | bytes 393216 | tf_op jit(solution)/shard_map/psum | solution.py:248
  316.2 14.8 %copy-start.14 = (f32[128,16]{0,1:T(8,128)S(1)}, f32[128,16]{0,1:T(8,128)}, u32[]{:S(2)}) copy-start(f32[128,16]{0,1:T(8,128)} %get-tuple-element.362) | copy-start | bytes 24580
  316.2 15.7 %copy-start.16 = (f32[128,16]{0,1:T(8,128)S(1)}, f32[128,16]{0,1:T(8,128)}, u32[]{:S(2)}) copy-start(f32[128,16]{0,1:T(8,128)} %copy-done.15) | copy-start | bytes 24580
  316.2 15.7 %copy-start.19 = (s32[128]{0:T(128)S(1)}, s32[128]{0:T(128)}, u32[]{:S(2)}) copy-start(s32[128]{0:T(128)} %param.27) | copy-start | bytes 1540
  (8 other events, 33.9 us)
Sparse Core Ops, SparseCore 0:
  10.6 80.4 all-gather.4
  110.7 19.6 reduce-scatter.3
  131.9 21.2 all-gather.6
  155.2 37.8 all-gather.8
  195.2 20.4 all-reduce.4
  217.7 37.8 all-gather.10
  263.6 8.9 reduce-scatter.7
  274.8 20.9 reduce-scatter.5
  332.0 91.9 all-reduce.6
